TPU v7x, 128 devices: a whole 4x4x4 slice. The times are simulated.
128 devices in a mesh: prompts: 1, model: 16 (over z, y), resp: 8 (over x, core).
Axes of the slice: x: 4, y: 4, z: 4, core: 2. Of those that a mesh axis runs over, the one named last changes fastest.
Arguments:
- x_prompt: bfloat16 [1024, 4096], P(('prompts', 'resp'))
- x_resp: bfloat16 [8, 1024, 4096], P(('prompts', 'resp'))
- targets: int32 [8, 1024], P(('prompts', 'resp'))
- resp_lens: int32 [8], P(('prompts', 'resp'))
- attn_gain: float32 [2, 4096], replicated
- w_query: bfloat16 [2, 4096, 32, 128], P(None, None, 'model')
- w_key: bfloat16 [2, 4096, 32, 128], P(None, None, 'model')
- w_value: bfloat16 [2, 4096, 32, 128], P(None, None, 'model')
- w_out: bfloat16 [2, 32, 128, 4096], P(None, 'model')
- mlp_gain: float32 [2, 4096], replicated
- w_gate: bfloat16 [2, 4096, 11008], P(None, None, 'model')
- w_up: bfloat16 [2, 4096, 11008], P(None, None, 'model')
- w_down: bfloat16 [2, 11008, 4096], P(None, 'model')
- final_gain: float32 [4096], replicated
- w_vocab: bfloat16 [4096, 32768], P(None, 'model')
Outputs:
- output: float32 [8, 1024], P(('prompts', 'resp'))
All inputs are finite; a program needn't handle non-finite values.
Results may differ from a plain program's by a relative error of at most 0.002451.
Values are sent between devices in bfloat16 or wider.
A program may use at most 1 GiB of HBM per device.

v0:
```python
import jax
import jax.numpy as jnp
from jax import lax
from jax.sharding import PartitionSpec as P

EPS = 1e-6
ROPE_BASE = 10000.0


def rms_norm(acts_in, gain_vec):
    acts_f = acts_in.astype(jnp.float32)
    inv_rms = lax.rsqrt(jnp.mean(acts_f * acts_f, axis=-1, keepdims=True) + EPS)
    return (acts_f * inv_rms * gain_vec).astype(jnp.bfloat16)


def rotary(projected, positions):
    half_dim = projected.shape[-1] // 2
    frequency = ROPE_BASE ** (-jnp.arange(half_dim, dtype=jnp.float32) / half_dim)
    angles = positions.astype(jnp.float32)[..., None] * frequency
    cos_part = jnp.cos(angles)[..., None, :]
    sin_part = jnp.sin(angles)[..., None, :]
    lower_half = projected[..., :half_dim]
    upper_half = projected[..., half_dim:]
    return jnp.concatenate([lower_half * cos_part - upper_half * sin_part, upper_half * cos_part + lower_half * sin_part], axis=-1)


def attend(queries, keys, values, query_pos, key_pos):
    heads, head_dim = queries.shape[-2], queries.shape[-1]
    kv_heads = keys.shape[-2]
    grouped = queries.reshape(queries.shape[:-2] + (kv_heads, heads // kv_heads, head_dim))
    scores = jnp.einsum('...tkrd,...skd->...krts', grouped, keys, preferred_element_type=jnp.float32) * (head_dim ** -0.5)
    visible = (key_pos[None, :] <= query_pos[..., :, None])[..., None, None, :, :]
    scores = jnp.where(visible, scores, -jnp.inf)
    row_max = jnp.max(scores, axis=-1, keepdims=True)
    exp_scores = jnp.exp(scores - row_max)
    row_sum = jnp.moveaxis(jnp.sum(exp_scores, axis=-1), -1, -3)
    mixed = jnp.einsum('...krts,...skd->...tkrd', exp_scores.astype(jnp.bfloat16), values, preferred_element_type=jnp.float32)
    return (mixed / row_sum[..., None]).reshape(queries.shape).astype(jnp.bfloat16)


def solution(mesh):
    groups = mesh.shape['resp']
    row_axes = ('prompts', 'resp')
    head_spec = P(None, None, 'model', None)
    in_specs = (P(row_axes, None), P(row_axes, None, None), P(row_axes, None), P(row_axes), P(None, None), head_spec, head_spec, head_spec, P(None, 'model', None, None), P(None, None), P(None, None, 'model'), P(None, None, 'model'), P(None, 'model', None), P(None), P(None, 'model'))

    def device_step(x_prompt, x_resp, targets, resp_lens, attn_gain, w_query, w_key, w_value, w_out, mlp_gain, w_gate, w_up, w_down, final_gain, w_vocab):
        prompt_rows = x_prompt.shape[0]
        resp_len = x_resp.shape[1]
        prompt_len = prompt_rows * groups
        num_layers = w_query.shape[0]
        resp_pos = prompt_len + jnp.arange(resp_len)
        tok_pos = jnp.concatenate([lax.axis_index('resp') * prompt_rows + jnp.arange(prompt_rows), resp_pos])
        key_pos = jnp.concatenate([jnp.arange(prompt_len), resp_pos])
        residual = jnp.concatenate([x_prompt, x_resp[0]], axis=0)
        for layer_idx in range(num_layers):
            hidden = rms_norm(residual, attn_gain[layer_idx])
            keys = rotary(jnp.einsum('td,dhe->the', hidden, w_key[layer_idx], preferred_element_type=jnp.float32), tok_pos).astype(jnp.bfloat16)
            values = jnp.einsum('td,dhe->the', hidden, w_value[layer_idx], preferred_element_type=jnp.float32).astype(jnp.bfloat16)
            prompt_keys = lax.all_gather(keys[:prompt_rows], 'resp', axis=0, tiled=True)
            prompt_values = lax.all_gather(values[:prompt_rows], 'resp', axis=0, tiled=True)
            all_keys = jnp.concatenate([prompt_keys, keys[prompt_rows:]], axis=0)
            all_values = jnp.concatenate([prompt_values, values[prompt_rows:]], axis=0)
            query_pos = tok_pos
            if layer_idx == num_layers - 1:
                residual = residual[prompt_rows:]
                hidden = hidden[prompt_rows:]
                query_pos = resp_pos
            queries = rotary(jnp.einsum('td,dhe->the', hidden, w_query[layer_idx], preferred_element_type=jnp.float32), query_pos).astype(jnp.bfloat16)
            mixed = attend(queries, all_keys, all_values, query_pos, key_pos)
            attn_part = jnp.einsum('the,hed->td', mixed, w_out[layer_idx], preferred_element_type=jnp.float32)
            residual = (residual.astype(jnp.float32) + lax.psum(attn_part, 'model')).astype(jnp.bfloat16)
            hidden = rms_norm(residual, mlp_gain[layer_idx])
            gate = jnp.dot(hidden, w_gate[layer_idx], preferred_element_type=jnp.float32)
            up_proj = jnp.dot(hidden, w_up[layer_idx], preferred_element_type=jnp.float32)
            inner = (jax.nn.silu(gate) * up_proj).astype(jnp.bfloat16)
            down_part = jnp.dot(inner, w_down[layer_idx], preferred_element_type=jnp.float32)
            residual = (residual.astype(jnp.float32) + lax.psum(down_part, 'model')).astype(jnp.bfloat16)
        logits = jnp.dot(rms_norm(residual, final_gain), w_vocab, preferred_element_type=jnp.float32)
        vocab_local = logits.shape[-1]
        vocab_ids = lax.axis_index('model') * vocab_local + jnp.arange(vocab_local)
        row_max = lax.pmax(jnp.max(logits, axis=-1), 'model')
        exp_total = lax.psum(jnp.sum(jnp.exp(logits - row_max[:, None]), axis=-1), 'model')
        picked = lax.psum(jnp.sum(jnp.where(vocab_ids[None, :] == targets[0][:, None], logits, 0.0), axis=-1), 'model')
        log_probs = picked - row_max - jnp.log(exp_total)
        log_probs = jnp.where(jnp.arange(resp_len) < resp_lens[0], log_probs, 0.0)
        return log_probs[None, :]

    return jax.shard_map(device_step, mesh=mesh, in_specs=in_specs, out_specs=P(row_axes, None), check_vma=False)
```

profile of v0, /device:TPU:8, one launch (start us, length us, event | category | flops | bytes accessed | tf_op | source)
XLA Modules:
  0.0 1368.9 jit_solution(14549115730225425299)
XLA Ops:
  16.1 10.9 fusion.5
  44.4 8.3 fusion.166
  56.9 6.7 copy.43
  63.6 8.2 fusion.165
  75.6 13.8 %all_gather.13 = bf16[1024,2,128]{0,2,1:T(8,128)(2,1)S(1)} all-gather(bf16[128,2,128]{0,2,1:T(8,128)(2,1)S(1)} %pad_maximum_fusion.2), channel_id=1, replica_groups=mesh['prompts'=1,'model'=16,'resp'=8] {'resp'}, dimensions={0}, use_global_device_ids=true | all-gather | bytes 589824 | tf_op jit(solution)/shard_map/all_gather | solution.py:60
  89.5 13.1 all_gather.12
  104.1 9.0 fusion.163
  113.0 8.8 fusion.18
  121.9 19.6 %convolution_bitcast_fusion = f32[1152,4096]{1,0:T(8,128)} fusion(bf16[2,2,128,4096]{3,2,1,0:T(8,128)(2,1)} %param.23, f32[2,1,1152,2048]{2,3,0,1:T(8,128)} %get-tuple-element.42, f32[2,1152]{1,0:T(2,128)S(1)} %get-tuple-element.41, bf16[1024,2,128]{2,0,1:T(8,128)(2,1)} %slice.145, bf16[1024,2,128]{2,0,1:T(8,128)(2,1)} %all_gather.12, ...), kind=kOutput, calls=%fused_computation.26 | convolution fusion | flops 3636002816 | bytes 40912896 | tf_op jit(solution)/shard_map/the,hed->td/dot_general | solution.py:71
  142.3 242.0 %all-reduce.6.cloned.1.call-done = f32[1152,4096]{1,0:T(8,128)} async-done(((f32[1152,4096]{1,0:T(8,128)}), f32[1152,4096]{1,0:T(8,128)}) %all-reduce.6.cloned.1.call-update) | async-done | bytes 18874384 | tf_op jit(solution)/shard_map/psum | solution.py:72
  384.3 10.1 fusion.7
  394.3 12.1 fusion.51
  406.5 10.3 fusion.62
  416.8 13.4 fusion.47
  442.9 228.0 %all-reduce.8.cloned.1.call-done = f32[1152,4096]{1,0:T(8,128)} async-done(((f32[1152,4096]{1,0:T(8,128)}), f32[1152,4096]{1,0:T(8,128)}) %all-reduce.8.cloned.1.call-update) | async-done | bytes 18874384 | tf_op jit(solution)/shard_map/psum | solution.py:78
  670.9 13.8 %fusion = (f32[1152]{0:T(1024)S(1)}, bf16[1152,4096]{1,0:T(8,128)(2,1)}) fusion(f32[1152,4096]{1,0:T(8,128)} %all-reduce.8.cloned.1.call-done, bf16[1152,4096]{1,0:T(8,128)(2,1)} %copy-done), kind=kLoop, calls=%fused_computation.13 | loop fusion | flops 28310400 | bytes 37753344 | tf_op jit(solution)/shard_map/reduce_sum | solution.py:12
  684.6 11.3 fusion.2
  696.0 7.0 fusion.79
  706.9 14.2 %all_gather.15 = bf16[1024,2,128]{0,2,1:T(8,128)(2,1)} all-gather(bf16[128,2,128]{0,2,1:T(8,128)(2,1)S(1)} %pad_maximum_fusion.1), channel_id=1, replica_groups=mesh['prompts'=1,'model'=16,'resp'=8] {'resp'}, dimensions={0}, use_global_device_ids=true | all-gather | bytes 589824 | tf_op jit(solution)/shard_map/all_gather | solution.py:60
  723.5 13.1 all_gather.14
  748.0 9.6 fusion.126
  757.6 8.1 convolution_bitcast_fusion.1
  766.0 219.4 %all-reduce.10.cloned.1.call-done = f32[1024,4096]{1,0:T(8,128)} async-done(((f32[1024,4096]{1,0:T(8,128)}), f32[1024,4096]{1,0:T(8,128)}) %all-reduce.10.cloned.1.call-update) | async-done | bytes 16777232 | tf_op jit(solution)/shard_map/psum | solution.py:72
  985.4 9.4 fusion.14
  994.8 10.5 fusion.45
  1005.3 8.3 fusion.43
  1013.7 10.4 fusion.41
  1024.8 219.4 %all-reduce.12.cloned.1.call-done = f32[1024,4096]{1,0:T(8,128)} async-done(((f32[1024,4096]{1,0:T(8,128)}), f32[1024,4096]{1,0:T(8,128)}) %all-reduce.12.cloned.1.call-update) | async-done | bytes 16777232 | tf_op jit(solution)/shard_map/psum | solution.py:78
  1244.2 9.1 fusion.11
  1253.3 27.8 %fusion.164 = (f32[1024]{0:T(1024)S(1)}, f32[1024,2048]{1,0:T(8,128)}) fusion(bf16[4096,2048]{1,0:T(8,128)(2,1)} %param.29, f32[4096]{0:T(1024)S(1)} %copy-done.18, f32[1024]{0:T(1024)S(1)} %add_rsqrt_fusion.3, f32[1024,4096]{1,0:T(8,128)} %all-reduce.12.cloned.1.call-done, bf16[1024,4096]{1,0:T(8,128)(2,1)} %copy-done.1), kind=kOutput, calls=%fused_computation.176 | convolution fusion | flops 17211326464 | bytes 50356224 | tf_op jit(solution)/shard_map/dot_general | solution.py:79
  1281.2 36.0 %pmax.7 = f32[1024]{0:T(1024)S(1)} all-reduce(f32[1024]{0:T(1024)S(1)} %get-tuple-element.45), channel_id=1, replica_groups=mesh['prompts'=1,'model'=16,'resp'=8] {'model'}, use_global_device_ids=true, to_apply=%region_16.17 | all-reduce | flops 1024 | bytes 8192 | tf_op jit(solution)/shard_map/pmax | solution.py:82
  1321.9 39.6 %all-reduce = (f32[1024]{0:T(1024)S(1)}, f32[1024]{0:T(1024)S(1)}) all-reduce(f32[1024]{0:T(1024)S(1)} %get-tuple-element.6, f32[1024]{0:T(1024)S(1)} %get-tuple-element.5), channel_id=1, replica_groups=mesh['prompts'=1,'model'=16,'resp'=8] {'model'}, use_global_device_ids=true, to_apply=%region_18.19 | all-reduce | flops 2048 | bytes 16384 | tf_op jit(solution)/shard_map/psum | solution.py:83
  (98 shorter events, 73.0 us)
Async XLA Ops:
  6.5 9.6 copy-start.4
  6.5 5.7 copy-start.15
  6.5 377.7 %all-reduce.6.cloned.1.call-start = ((), (), s32[]{:S(2)}) async-start(), calls=%async_computation | async-start | bytes 37748736 | tf_op jit(solution)/shard_map/psum | solution.py:72
  6.5 5.7 copy-start.6
  27.0 7.4 copy-start.7
  33.5 4.7 copy-start.13
  44.4 8.3 copy-start.8
  63.6 25.9 %slice-start.3 = ((bf16[1152,2,128]{2,0,1:T(8,128)(2,1)}), bf16[128,2,128]{2,0,1:T(8,128)(2,1)S(1)}, s32[]{:S(2)}) async-start(bf16[1152,2,128]{2,0,1:T(8,128)(2,1)} %copy-done.13), calls=%async_computation.7 | async-start | bytes 131072 | tf_op jit(solution)/shard_map/slice | solution.py:61
  73.0 0.7 copy-start.9
  141.5 0.8 copy-start.16
  141.5 529.4 %all-reduce.8.cloned.1.call-start = ((), (), s32[]{:S(2)}) async-start(), calls=%async_computation.1 | async-start | bytes 37748736 | tf_op jit(solution)/shard_map/psum | solution.py:78
  394.3 12.2 copy-start
  430.2 555.2 %all-reduce.10.cloned.1.call-start = ((), (), s32[]{:S(2)}) async-start(), calls=%async_computation.2 | async-start | bytes 33554432 | tf_op jit(solution)/shard_map/psum | solution.py:72
  696.0 7.1 copy-start.3
  696.0 7.6 copy-start.12
  703.0 3.7 copy-start.14
  703.5 3.2 copy-start.10
  703.5 17.6 %copy-start.11 = (bf16[1,4096,2,128]{1,3,2,0:T(8,128)(2,1)S(1)}, bf16[1,4096,2,128]{1,3,2,0:T(8,128)(2,1)}, u32[]{:S(2)}) copy-start(bf16[1,4096,2,128]{1,3,2,0:T(8,128)(2,1)} %copy.47) | copy-start | bytes 6291460
  721.1 2.4 slice-start.4
  742.2 5.7 copy-start.2
  742.2 5.7 slice-start.5
  748.0 9.6 copy-start.5
  765.8 478.4 %all-reduce.12.cloned.1.call-start = ((), (), s32[]{:S(2)}) async-start(), calls=%async_computation.3 | async-start | bytes 33554432 | tf_op jit(solution)/shard_map/psum | solution.py:78
  994.8 10.5 copy-start.1
  994.8 18.9 %slice-start = ((s8[11272192]{0:T(1024)(128)(4,1)}), s8[4194304]{0:T(1024)(128)(4,1)S(1)}, s32[]{:S(2)}) async-start(s8[11272192]{0:T(1024)(128)(4,1)} %bitcast.167), calls=%async_computation.4 | async-start | bytes 8388608
  994.8 18.9 %slice-start.1 = ((s8[11272192]{0:T(1024)(128)(4,1)}), s8[4194304]{0:T(1024)(128)(4,1)S(1)}, s32[]{:S(2)}) async-start(s8[11272192]{0:T(1024)(128)(4,1)} %bitcast.167), calls=%async_computation.5 | async-start | bytes 8388608
  1005.3 8.4 slice-start.2
  1024.7 228.6 %copy-start.18 = (f32[4096]{0:T(1024)S(1)}, f32[4096]{0:T(1024)}, u32[]{:S(2)}) copy-start(f32[4096]{0:T(1024)} %param.28) | copy-start | bytes 49156
  1253.3 63.8 %copy-start.17 = (s32[1,1024]{1,0:T(1,128)S(1)}, s32[1,1024]{1,0:T(1,128)}, u32[]{:S(2)}) copy-start(s32[1,1024]{1,0:T(1,128)} %param.17) | copy-start | bytes 12292
Sparse Core Ops, SparseCore 0:
  141.6 242.5 all-reduce.5
  430.3 240.5 all-reduce.7
  765.9 219.4 all-reduce.9
  1024.2 219.9 all-reduce.11
where the time goes:
time: 1380 us; the launch traced here: 1370 us
  waiting for transfers between devices  909 us (66%)
  matrix products  179 us (13%)
  blocking collectives  130 us (9%)
  other arithmetic  96.2 us (7%)
  local copies, waits for them, and re-layouts  39.7 us (3%)
  between operations  14.5 us (1%)
    psum x2, waiting for transfers between devices, device_step(): lax.psum(attn_part, 'model')  461 us
    psum x2, waiting for transfers between devices, device_step(): lax.psum(down_part, 'model')  447 us
    reduce_sum x5, other arithmetic, rms_norm(): inv_rms = lax.rsqrt(jnp.mean(acts_f * acts_f, axis=-1, keepdims=True) + EPS)  48 us
    psum x1, blocking collectives, device_step(): lax.psum(jnp.sum(jnp.exp(logits - row_max[:, None]), axis=-1), 'model')  39.6 us
    pmax x1, blocking collectives, device_step(): row_max = lax.pmax(jnp.max(logits, axis=-1), 'model')  36 us
    all_gather x2, blocking collectives, device_step(): prompt_keys = lax.all_gather(keys[:prompt_rows], 'resp', axis=0, tiled=True)  28 us
    dot_general x1, matrix products, device_step(): jnp.dot(rms_norm(residual, final_gain), w_vocab, preferred_element_type=j...  27.8 us
    dot_general x2, matrix products, device_step(): jnp.einsum('the,hed->td', mixed, w_out[layer_idx], preferred_element_type...  27.7 us
  transfers between devices with their start and end apart: 4, of which 4 were waited for; matrix products, arithmetic and copies ran while one was open for 1% of the time, Pallas kernels for 0%

commit v1 on v0

v1 whole, which is shorter than its diff:
```python
import jax
import jax.numpy as jnp
from jax import lax
from jax.sharding import PartitionSpec as P

EPS = 1e-6
ROPE_BASE = 10000.0


def rms_norm(acts_in, gain_vec):
    acts_f = acts_in.astype(jnp.float32)
    inv_rms = lax.rsqrt(jnp.mean(acts_f * acts_f, axis=-1, keepdims=True) + EPS)
    return (acts_f * inv_rms * gain_vec).astype(jnp.bfloat16)


def rope_tables(positions, half_dim):
    frequency = ROPE_BASE ** (-jnp.arange(half_dim, dtype=jnp.float32) / half_dim)
    angles = positions.astype(jnp.float32)[..., None] * frequency
    return jnp.cos(angles)[..., None, :], jnp.sin(angles)[..., None, :]


def rotary(projected, tables):
    cos_part, sin_part = tables
    half_dim = projected.shape[-1] // 2
    lower_half = projected[..., :half_dim]
    upper_half = projected[..., half_dim:]
    return jnp.concatenate([lower_half * cos_part - upper_half * sin_part, upper_half * cos_part + lower_half * sin_part], axis=-1)


def attend(queries, keys, values, query_pos, key_pos):
    head_dim = queries.shape[-1]
    scores = jnp.einsum('the,she->hts', queries, keys, preferred_element_type=jnp.float32) * (head_dim ** -0.5)
    visible = (key_pos[None, :] <= query_pos[:, None])[None]
    scores = jnp.where(visible, scores, -jnp.inf)
    row_max = jnp.max(scores, axis=-1, keepdims=True)
    exp_scores = jnp.exp(scores - row_max)
    row_sum = jnp.moveaxis(jnp.sum(exp_scores, axis=-1), -1, 0)
    mixed = jnp.einsum('hts,she->the', exp_scores.astype(jnp.bfloat16), values, preferred_element_type=jnp.float32)
    return (mixed / row_sum[..., None]).astype(jnp.bfloat16)


def solution(mesh):
    groups = mesh.shape['resp']
    shards = mesh.shape['model']
    row_axes = ('prompts', 'resp')
    head_spec = P(None, None, 'model', None)
    in_specs = (P(row_axes, None), P(row_axes, None, None), P(row_axes, None), P(row_axes), P(None, None), head_spec, head_spec, head_spec, P(None, 'model', None, None), P(None, None), P(None, None, 'model'), P(None, None, 'model'), P(None, 'model', None), P(None), P(None, 'model'))

    def device_step(x_prompt, x_resp, targets, resp_lens, attn_gain, w_query, w_key, w_value, w_out, mlp_gain, w_gate, w_up, w_down, final_gain, w_vocab):
        prompt_rows = x_prompt.shape[0]
        resp_len = x_resp.shape[1]
        width = x_resp.shape[2]
        prompt_len = prompt_rows * groups
        num_layers = w_query.shape[0]
        part_p, part_r = prompt_rows // shards, resp_len // shards
        me = lax.axis_index('model')
        resp_pos = prompt_len + jnp.arange(resp_len)
        prompt_pos = lax.axis_index('resp') * prompt_rows + jnp.arange(prompt_rows)
        mine = lambda rows, n: lax.dynamic_slice_in_dim(rows, me * n, n, 0)
        residual = jnp.concatenate([mine(x_prompt, part_p), mine(x_resp[0], part_r)], axis=0)
        hidden = jnp.concatenate([x_prompt.reshape(shards, part_p, width), x_resp[0].reshape(shards, part_r, width)], axis=1).reshape(-1, width)
        hidden = rms_norm(hidden, attn_gain[0])
        tok_pos = jnp.concatenate([prompt_pos.reshape(shards, part_p), resp_pos.reshape(shards, part_r)], axis=1).reshape(-1)
        key_pos = jnp.concatenate([jnp.arange(prompt_len), resp_pos])

        def reduce_rows(part):
            return lax.psum_scatter(part, 'model', scatter_dimension=0, tiled=True)

        def gather_rows(rows):
            return lax.all_gather(rows, 'model', axis=0, tiled=True)

        def split(rows):
            cut = rows.reshape((shards, part_p + part_r) + rows.shape[1:])
            return cut[:, :part_p].reshape((prompt_rows,) + rows.shape[1:]), cut[:, part_p:].reshape((resp_len,) + rows.shape[1:])

        for layer_idx in range(num_layers):
            tables = rope_tables(tok_pos, w_key.shape[-1] // 2)
            keys = rotary(jnp.einsum('td,dhe->the', hidden, w_key[layer_idx], preferred_element_type=jnp.float32), tables).astype(jnp.bfloat16)
            values = jnp.einsum('td,dhe->the', hidden, w_value[layer_idx], preferred_element_type=jnp.float32).astype(jnp.bfloat16)
            key_p, key_r = split(keys)
            val_p, val_r = split(values)
            both = lax.all_gather(jnp.concatenate([key_p, val_p], axis=1), 'resp', axis=0, tiled=True)
            heads = keys.shape[1]
            all_keys = jnp.concatenate([both[:, :heads], key_r], axis=0)
            all_values = jnp.concatenate([both[:, heads:], val_r], axis=0)
            query_pos = tok_pos
            if layer_idx == num_layers - 1:
                residual = residual[part_p:]
                hidden = split(hidden)[1]
                query_pos = resp_pos
                tables = rope_tables(query_pos, w_key.shape[-1] // 2)
            queries = rotary(jnp.einsum('td,dhe->the', hidden, w_query[layer_idx], preferred_element_type=jnp.float32), tables).astype(jnp.bfloat16)
            mixed = attend(queries, all_keys, all_values, query_pos, key_pos)
            attn_part = jnp.einsum('the,hed->td', mixed, w_out[layer_idx], preferred_element_type=jnp.float32)
            residual = (residual.astype(jnp.float32) + reduce_rows(attn_part)).astype(jnp.bfloat16)
            hidden = gather_rows(rms_norm(residual, mlp_gain[layer_idx]))
            gate = jnp.dot(hidden, w_gate[layer_idx], preferred_element_type=jnp.float32)
            up_proj = jnp.dot(hidden, w_up[layer_idx], preferred_element_type=jnp.float32)
            inner = (jax.nn.silu(gate) * up_proj).astype(jnp.bfloat16)
            down_part = jnp.dot(inner, w_down[layer_idx], preferred_element_type=jnp.float32)
            residual = (residual.astype(jnp.float32) + reduce_rows(down_part)).astype(jnp.bfloat16)
            next_gain = attn_gain[layer_idx + 1] if layer_idx < num_layers - 1 else final_gain
            hidden = gather_rows(rms_norm(residual, next_gain))
        logits = jnp.dot(hidden, w_vocab, preferred_element_type=jnp.float32)
        vocab_local = logits.shape[-1]
        vocab_ids = me * vocab_local + jnp.arange(vocab_local)
        row_max = jnp.max(logits, axis=-1)
        exp_total = jnp.sum(jnp.exp(logits - row_max[:, None]), axis=-1)
        picked = jnp.sum(jnp.where(vocab_ids[None, :] == targets[0][:, None], logits, 0.0), axis=-1)
        stats = lax.all_gather(jnp.stack([row_max, exp_total, picked]), 'model', axis=0)
        top = jnp.max(stats[:, 0], axis=0)
        total = jnp.sum(stats[:, 1] * jnp.exp(stats[:, 0] - top), axis=0)
        log_probs = jnp.sum(stats[:, 2], axis=0) - top - jnp.log(total)
        log_probs = jnp.where(jnp.arange(resp_len) < resp_lens[0], log_probs, 0.0)
        return log_probs[None, :]

    return jax.shard_map(device_step, mesh=mesh, in_specs=in_specs, out_specs=P(row_axes, None), check_vma=False)
```

time: 1380 us -> 1100 us (0.80)
  the two profiles are of different devices: /device:TPU:8 before, /device:TPU:1 now
where the time goes in v1:
time: 1100 us; the launch traced here: 1090 us
  waiting for transfers between devices  769 us (70%)
  matrix products  167 us (15%)
  local copies, waits for them, and re-layouts  63.4 us (6%)
  other arithmetic  55.3 us (5%)
  blocking collectives  18.2 us (2%)
  between operations  15.1 us (1%)
    all_gather x4, waiting for transfers between devices, gather_rows(): return lax.all_gather(rows, 'model', axis=0, tiled=True)  287 us
    unnamed x12, waiting for transfers between devices  240 us
    reduce_scatter x2, waiting for transfers between devices, reduce_rows(): return lax.psum_scatter(part, 'model', scatter_dimension=0, tiled=True)  220 us
    unnamed x4, matrix products  25.3 us
    dot_general x1, matrix products, device_step(): logits = jnp.dot(hidden, w_vocab, preferred_element_type=jnp.float32)  23.2 us
  transfers between devices with their start and end apart: 10, of which 9 were waited for; matrix products, arithmetic and copies ran while one was open for 4% of the time, Pallas kernels for 0%

profile of v1, /device:TPU:1, one launch (start us, length us, event | category | flops | bytes accessed | tf_op | source)
XLA Modules:
  0.0 1088.0 jit_solution(10779029129519088639)
XLA Ops:
  6.6 5.7 fusion
  20.0 5.8 fusion.114
  29.7 8.6 fusion.2
  38.4 7.8 fusion.122
  57.4 6.0 fusion.115
  63.4 6.3 convolution_convert_fusion
  75.8 21.4 %all-gather.9.cloned.1.call-done = bf16[1024,4,128]{2,0,1:T(8,128)(2,1)} async-done(((bf16[128,4,128]{2,0,1:T(8,128)(2,1)}), bf16[1024,4,128]{2,0,1:T(8,128)(2,1)}) %all-gather.9.cloned.1.call-update) | async-done | bytes 1048592 | tf_op jit(solution)/shard_map/all_gather | solution.py:82
  99.3 10.2 fusion.3
  109.6 10.3 fusion.5
  122.1 6.4 fusion.50
  128.5 9.5 convolution_bitcast_fusion
  139.2 119.4 %reduce-scatter.13.cloned.1.call-done = f32[72,4096]{1,0:T(8,128)} async-done(((f32[1152,4096]{1,0:T(8,128)}), f32[72,4096]{1,0:T(8,128)}) %reduce-scatter.13.cloned.1.call-update) | async-done | bytes 1179664
  261.2 75.3 %all-gather.11.cloned.1.call-done = bf16[1152,4096]{1,0:T(8,128)(2,1)} async-done(((bf16[72,4096]{1,0:T(8,128)(2,1)}), bf16[1152,4096]{1,0:T(8,128)(2,1)}) %all-gather.11.cloned.1.call-update) | async-done | bytes 9437200 | tf_op jit(solution)/shard_map/all_gather | solution.py:70
  336.6 11.3 %fusion.27 = f32[1152,688]{0,1:T(8,128)S(1)} fusion(bf16[1152,4096]{1,0:T(8,128)(2,1)} %all-gather.11.cloned.1.call-done, bf16[2,4096,688]{1,2,0:T(8,128)(2,1)} %param.25), kind=kOutput, calls=%fused_computation.36 | convolution fusion | flops 6492782592 | bytes 18243584 | tf_op jit(solution)/shard_map/dot_general | solution.py:97
  347.9 9.8 fusion.38
  357.8 10.7 fusion.23
  368.5 120.9 %reduce-scatter.15.cloned.1.call-done = f32[72,4096]{1,0:T(8,128)} async-done(((f32[1152,4096]{1,0:T(8,128)}), f32[72,4096]{1,0:T(8,128)}) %reduce-scatter.15.cloned.1.call-update) | async-done | bytes 1179664
  497.0 71.2 %all-gather.13.cloned.1.call-done = bf16[1152,4096]{1,0:T(8,128)(2,1)} async-done(((bf16[72,4096]{1,0:T(8,128)(2,1)}), bf16[1152,4096]{1,0:T(8,128)(2,1)}) %all-gather.13.cloned.1.call-update) | async-done | bytes 9437200 | tf_op jit(solution)/shard_map/all_gather | solution.py:70
  568.2 7.2 fusion.123
  578.4 7.0 fusion.44
  597.8 7.9 slice.184
  607.4 6.4 fusion.124
  630.4 8.6 convolution_bitcast_fusion.1
  639.1 109.9 %reduce-scatter.9.cloned.1.call-done = f32[64,4096]{1,0:T(8,128)} async-done(((f32[1024,4096]{1,0:T(8,128)}), f32[64,4096]{1,0:T(8,128)}) %reduce-scatter.9.cloned.1.call-update) | async-done | bytes 1048592 | tf_op jit(solution)/shard_map/reduce_scatter | solution.py:67
  751.6 70.7 %all-gather.17.cloned.1.call-done = bf16[1024,4096]{1,0:T(8,128)(2,1)} async-done(((bf16[64,4096]{1,0:T(8,128)(2,1)}), bf16[1024,4096]{1,0:T(8,128)(2,1)}) %all-gather.17.cloned.1.call-update) | async-done | bytes 8388624 | tf_op jit(solution)/shard_map/all_gather | solution.py:70
  822.4 10.2 fusion.19
  832.6 8.6 multiply_convert_fusion
  841.3 10.3 fusion.17
  851.7 110.0 %reduce-scatter.11.cloned.1.call-done = f32[64,4096]{1,0:T(8,128)} async-done(((f32[1024,4096]{1,0:T(8,128)}), f32[64,4096]{1,0:T(8,128)}) %reduce-scatter.11.cloned.1.call-update) | async-done | bytes 1048592 | tf_op jit(solution)/shard_map/reduce_scatter | solution.py:67
  966.1 70.0 %all-gather.19.cloned.1.call-done = bf16[1024,4096]{1,0:T(8,128)(2,1)} async-done(((bf16[64,4096]{1,0:T(8,128)(2,1)}), bf16[1024,4096]{1,0:T(8,128)(2,1)}) %all-gather.19.cloned.1.call-update) | async-done | bytes 8388624 | tf_op jit(solution)/shard_map/all_gather | solution.py:70
  1036.1 23.2 %fusion.120 = (f32[1024]{0:T(1024)S(1)}, f32[1024,2048]{1,0:T(8,128)S(1)}) fusion(bf16[1024,4096]{1,0:T(8,128)(2,1)} %all-gather.19.cloned.1.call-done, bf16[4096,2048]{1,0:T(8,128)(2,1)} %param.29), kind=kOutput, calls=%fused_computation.168 | convolution fusion | flops 17181966336 | bytes 33558528 | tf_op jit(solution)/shard_map/dot_general | solution.py:104
  1061.9 18.2 %all-gather.1 = f32[16,3,1024]{2,1,0:T(4,128)S(1)} all-gather(f32[1,3,1024]{2,1,0:T(4,128)S(1)} %maximum_bitcast_fusion), channel_id=2, replica_groups=mesh['prompts'=1,'model'=16,'resp'=8] {'model'}, dimensions={0}, use_global_device_ids=true | all-gather | bytes 208896 | tf_op jit(solution)/shard_map/all_gather | solution.py:110
  (163 shorter events, 88.0 us)
Async XLA Ops:
  6.5 90.7 %all-gather.9.cloned.1.call-start = ((), (), s32[]{:S(2)}) async-start(), calls=%async_computation.4 | async-start | bytes 1179648 | tf_op jit(solution)/shard_map/all_gather | solution.py:82
  20.0 9.7 copy-start.7
  29.7 8.6 copy-start.14
  38.4 7.8 copy-start.2
  38.4 7.8 copy-start.15
  70.5 188.0 %reduce-scatter.13.cloned.1.call-start = ((), (), s32[]{:S(2)}) async-start(), calls=%async_computation.12 | async-start | bytes 20054016
  75.8 33.8 %copy-start.1 = (pred[1152,2048]{1,0:T(8,128)(4,1)}, pred[1152,2048]{1,0:T(8,128)(4,1)S(1)}, u32[]{:S(2)}) copy-start(pred[1152,2048]{1,0:T(8,128)(4,1)S(1)} %broadcast_compare_fusion) | copy-start | bytes 7077892
  109.6 12.5 %copy-start = (f32[2,1152,2048]{2,1,0:T(8,128)S(1)}, f32[2,1152,2048]{2,1,0:T(8,128)}, u32[]{:S(2)}) copy-start(f32[2,1152,2048]{2,1,0:T(8,128)} %get-tuple-element.46) | copy-start | bytes 56623108
  138.0 198.6 %all-gather.11.cloned.1.call-start = ((), (), s32[]{:S(2)}) async-start(), calls=%async_computation.5 | async-start | bytes 10027008 | tf_op jit(solution)/shard_map/all_gather | solution.py:70
  261.2 228.2 %reduce-scatter.15.cloned.1.call-start = ((), (), s32[]{:S(2)}) async-start(), calls=%async_computation.13 | async-start | bytes 20054016
  336.6 11.3 %copy-start.26 = (bf16[1152,4096]{1,0:T(8,128)(2,1)S(1)}, bf16[1152,4096]{1,0:T(8,128)(2,1)}, u32[]{:S(2)}) copy-start(bf16[1152,4096]{1,0:T(8,128)(2,1)} %all-gather.11.cloned.1.call-done) | copy-start | bytes 28311556
  336.6 21.2 %slice-start = ((s8[11272192]{0:T(1024)(128)(4,1)}), s8[4194304]{0:T(1024)(128)(4,1)S(1)}, s32[]{:S(2)}) async-start(s8[11272192]{0:T(1024)(128)(4,1)} %bitcast.189), calls=%async_computation.14 | async-start | bytes 8388608
  336.6 21.2 %slice-start.1 = ((s8[11272192]{0:T(1024)(128)(4,1)}), s8[4194304]{0:T(1024)(128)(4,1)S(1)}, s32[]{:S(2)}) async-start(s8[11272192]{0:T(1024)(128)(4,1)} %bitcast.189), calls=%async_computation.15 | async-start | bytes 8388608
  347.9 9.9 slice-start.2
  368.4 124.4 %copy-start.4 = (bf16[1,4096,2,128]{3,2,1,0:T(2,128)(2,1)S(1)}, bf16[1,4096,2,128]{3,2,1,0:T(2,128)(2,1)}, u32[]{:S(2)}) copy-start(bf16[1,4096,2,128]{3,2,1,0:T(2,128)(2,1)} %get-tuple-element.17) | copy-start | bytes 6291460
  368.5 199.7 %all-gather.13.cloned.1.call-start = ((), (), s32[]{:S(2)}) async-start(), calls=%async_computation.6 | async-start | bytes 10027008 | tf_op jit(solution)/shard_map/all_gather | solution.py:70
  492.8 121.9 %all-gather.15.cloned.1.call-start = ((), (), s32[]{:S(2)}) async-start(), calls=%async_computation.7 | async-start | bytes 1179648 | tf_op jit(solution)/shard_map/all_gather | solution.py:82
  568.2 7.3 copy-start.13
  578.4 8.6 copy-start.3
  587.0 162.0 %reduce-scatter.9.cloned.1.call-start = ((), (), s32[]{:S(2)}) async-start(), calls=%async_computation.8 | async-start | bytes 17825792 | tf_op jit(solution)/shard_map/reduce_scatter | solution.py:67
  597.8 7.9 copy-start.9
  607.4 8.6 copy-start.20
  639.0 110.0 %copy-start.6 = (bf16[72,4096]{1,0:T(8,128)(2,1)S(1)}, bf16[72,4096]{1,0:T(8,128)(2,1)}, u32[]{:S(2)}) copy-start(bf16[72,4096]{1,0:T(8,128)(2,1)} %copy-done.5) | copy-start | bytes 1769476
  639.0 183.3 %all-gather.17.cloned.1.call-start = ((), (), s32[]{:S(2)}) async-start(), calls=%async_computation.9 | async-start | bytes 8912896 | tf_op jit(solution)/shard_map/all_gather | solution.py:70
  751.6 210.0 %reduce-scatter.11.cloned.1.call-start = ((), (), s32[]{:S(2)}) async-start(), calls=%async_computation.10 | async-start | bytes 17825792 | tf_op jit(solution)/shard_map/reduce_scatter | solution.py:67
  822.3 10.3 copy-start.27
  822.3 18.9 %slice-start.3 = ((s8[11272192]{0:T(1024)(128)(4,1)}), s8[4194304]{0:T(1024)(128)(4,1)S(1)}, s32[]{:S(2)}) async-start(s8[11272192]{0:T(1024)(128)(4,1)} %bitcast.191), calls=%async_computation.17 | async-start | bytes 8388608
  822.4 18.9 %slice-start.4 = ((s8[11272192]{0:T(1024)(128)(4,1)}), s8[4194304]{0:T(1024)(128)(4,1)S(1)}, s32[]{:S(2)}) async-start(s8[11272192]{0:T(1024)(128)(4,1)} %bitcast.191), calls=%async_computation.18 | async-start | bytes 8388608
  832.6 8.6 slice-start.5
  851.6 111.5 %copy-start.24 = (f32[4096]{0:T(1024)S(1)}, f32[4096]{0:T(1024)}, u32[]{:S(2)}) copy-start(f32[4096]{0:T(1024)} %param.28) | copy-start | bytes 49156
  851.6 184.5 %all-gather.19.cloned.1.call-start = ((), (), s32[]{:S(2)}) async-start(), calls=%async_computation.11 | async-start | bytes 8912896 | tf_op jit(solution)/shard_map/all_gather | solution.py:70
  966.1 93.2 %copy-start.25 = (s32[1,1024]{1,0:T(1,128)S(1)}, s32[1,1024]{1,0:T(1,128)}, u32[]{:S(2)}) copy-start(s32[1,1024]{1,0:T(1,128)} %param.17) | copy-start | bytes 12292
  (12 other events, 44.0 us)
Sparse Core Ops, SparseCore 0:
  70.6 26.6 all-gather.8
  138.1 120.4 reduce-scatter.12
  261.3 75.2 all-gather.10
  368.6 120.7 reduce-scatter.14
  492.9 75.2 all-gather.12
  587.1 23.2 all-gather.14
  639.2 109.8 reduce-scatter.8
  751.7 70.5 all-gather.16
  851.7 109.8 reduce-scatter.10
  965.5 70.5 all-gather.18

commit v2 on v1

v2 whole, which is shorter than its diff:
```python
import functools

import jax
import jax.numpy as jnp
from jax import lax
from jax.experimental import pallas as pl
from jax.experimental.pallas import tpu as pltpu

MESH = pl.DeviceIdType.MESH
F32 = jnp.float32
BF16 = jnp.bfloat16
EPS = 1e-6
N_KINDS = 24


def block_of(color, first, second):
    return 4 * second + first if color == 0 else 4 * first + second


class Torus:
    def __init__(self, refs, send_sem, recv_sem):
        self.st2, self.sb, self.r1, self.r2a, self.r2b, self.r3, self.r4, self.xg = refs
        self.send_sem, self.recv_sem = send_sem, recv_sem
        me = lax.axis_index("model")
        z, y = me // 4, me % 4
        self.place = ((y, z), (z, y))
        plus = lambda v, d: (v + d + 4) % 4
        self.plus = plus
        along_y = (z * 4 + plus(y, 1), z * 4 + plus(y, -1))
        along_z = (plus(z, 1) * 4 + y, plus(z, -1) * 4 + y)
        self.near = ((along_y, along_z), (along_z, along_y))
        self.all_near = along_y + along_z

    def barrier(self):
        sem = pltpu.get_barrier_semaphore()
        for device in self.all_near:
            pl.semaphore_signal(sem, inc=1, device_id={"model": device}, device_id_type=MESH)
        pl.semaphore_wait(sem, 4)

    def copy(self, kind, c, q, src, dst, device):
        return pltpu.make_async_remote_copy(
            src_ref=src, dst_ref=dst, send_sem=self.send_sem.at[c, q, kind], recv_sem=self.recv_sem.at[c, q, kind],
            device_id={"model": device}, device_id_type=MESH)

    def outgoing(self, kind, c, q):
        (p, s), plus = self.place[q], self.plus
        (right_p, left_p), (right_s, left_s) = self.near[q]
        st2, sb, r1, r2a, r2b, r3, r4, xg = (ref.at[c, q] for ref in (self.st2, self.sb, self.r1, self.r2a, self.r2b, self.r3, self.r4, self.xg))
        lo, hi = pl.ds(0, 2), pl.ds(2, 2)
        src, dst, device = {
            0: lambda: (st2.at[lo], r1.at[0], right_p),
            1: lambda: (st2.at[hi], r1.at[1], left_p),
            2: lambda: (sb.at[0], r2a.at[hi], right_p),
            3: lambda: (sb.at[1], r2b.at[lo], left_p),
            4: lambda: (r1.at[0], r2a.at[lo], right_p),
            5: lambda: (r1.at[1], r2b.at[hi], left_p),
            6: lambda: (r2a.at[plus(s, 2), 0], r3.at[0], right_s),
            7: lambda: (r2a.at[plus(s, 2), 1], r3.at[1], left_s),
            8: lambda: (r2a.at[plus(s, 1), 1], r4.at[0, 1], right_s),
            9: lambda: (r2a.at[plus(s, -1), 0], r4.at[1, 0], left_s),
            10: lambda: (r3.at[0], r4.at[0, 0], right_s),
            11: lambda: (r3.at[1], r4.at[1, 1], left_s),
            12: lambda: (xg.at[p, s, 0], xg.at[p, s, 0], right_s),
            13: lambda: (xg.at[p, s, 1], xg.at[p, s, 1], left_s),
            14: lambda: (xg.at[p, s, 1], xg.at[p, s, 1], right_s),
            15: lambda: (xg.at[p, s, 0], xg.at[p, s, 0], left_s),
            16: lambda: (xg.at[p, plus(s, -1), 0], xg.at[p, plus(s, -1), 0], right_s),
            17: lambda: (xg.at[p, plus(s, 1), 1], xg.at[p, plus(s, 1), 1], left_s),
            18: lambda: (xg.at[p, lo], xg.at[p, lo], right_p),
            19: lambda: (xg.at[p, hi], xg.at[p, hi], left_p),
            20: lambda: (xg.at[p, hi], xg.at[p, hi], right_p),
            21: lambda: (xg.at[p, lo], xg.at[p, lo], left_p),
            22: lambda: (xg.at[plus(p, -1), lo], xg.at[plus(p, -1), lo], right_p),
            23: lambda: (xg.at[plus(p, 1), hi], xg.at[plus(p, 1), hi], left_p),
        }[kind]()
        return self.copy(kind, c, q, src, dst, device)

    def incoming(self, kind, c, q):
        (p, s), plus = self.place[q], self.plus
        r1, r2a, r2b, r3, r4, xg = (ref.at[c, q] for ref in (self.r1, self.r2a, self.r2b, self.r3, self.r4, self.xg))
        lo, hi = pl.ds(0, 2), pl.ds(2, 2)
        (right_p, left_p), (right_s, left_s) = self.near[q]
        dst = {
            0: lambda: r1.at[0], 1: lambda: r1.at[1],
            2: lambda: r2a.at[hi], 3: lambda: r2b.at[lo], 4: lambda: r2a.at[lo], 5: lambda: r2b.at[hi],
            6: lambda: r3.at[0], 7: lambda: r3.at[1],
            8: lambda: r4.at[0, 1], 9: lambda: r4.at[1, 0], 10: lambda: r4.at[0, 0], 11: lambda: r4.at[1, 1],
            12: lambda: xg.at[p, plus(s, -1), 0], 13: lambda: xg.at[p, plus(s, 1), 1],
            14: lambda: xg.at[p, plus(s, -1), 1], 15: lambda: xg.at[p, plus(s, 1), 0],
            16: lambda: xg.at[p, plus(s, 2), 0], 17: lambda: xg.at[p, plus(s, 2), 1],
            18: lambda: xg.at[plus(p, -1), lo], 19: lambda: xg.at[plus(p, 1), hi],
            20: lambda: xg.at[plus(p, -1), hi], 21: lambda: xg.at[plus(p, 1), lo],
            22: lambda: xg.at[plus(p, 2), lo], 23: lambda: xg.at[plus(p, 2), hi],
        }[kind]()
        return self.copy(kind, c, q, dst, dst, right_p)

    def send(self, c, q, *kinds):
        for kind in kinds:
            self.outgoing(kind, c, q).start()

    def sent(self, c, q, *kinds):
        for kind in kinds:
            self.outgoing(kind, c, q).wait_send()

    def arrived(self, c, q, *kinds):
        for kind in kinds:
            self.incoming(kind, c, q).wait_recv()


def store_block(ref, value):
    ref[0] = value[:, :128]
    ref[1] = value[:, 128:]


def add_block(ref, value):
    ref[0] += value[:, :128]
    ref[1] += value[:, 128:]


def product(lhs, w_ref, color, first, second):
    start = pl.multiple_of(block_of(color, first, second) * 256, 256)
    return jnp.dot(lhs, w_ref[:, pl.ds(start, 256)], preferred_element_type=F32)


def stage_head(net, c, q, lhs, w_ref):
    (p, s), plus = net.place[q], net.plus
    for k in range(4):
        store_block(net.st2.at[c, q, k], product(lhs, w_ref, q, plus(p, 2), k))
    net.send(c, q, 0, 1)
    for k in range(2):
        store_block(net.sb.at[c, q, 0, k], product(lhs, w_ref, q, plus(p, 1), 2 + k))
        store_block(net.sb.at[c, q, 1, k], product(lhs, w_ref, q, plus(p, -1), k))
    net.send(c, q, 2, 3)


def stage_rest(net, chunks, lhs_of, w_ref, finish):
    plus = net.plus

    def over_chunks(body):
        @pl.loop(0, chunks)
        def _(c):
            for q in range(2):
                body(c, q)

    def relay_first(c, q):
        p, s = net.place[q]
        lhs = lhs_of(c, q)
        net.arrived(c, q, 0)
        for k in range(2):
            add_block(net.r1.at[c, q, 0, k], product(lhs, w_ref, q, plus(p, 1), k))
        net.send(c, q, 4)
        net.arrived(c, q, 1)
        for k in range(2):
            add_block(net.r1.at[c, q, 1, k], product(lhs, w_ref, q, plus(p, -1), 2 + k))
        net.send(c, q, 5)

    def own_first(c, q):
        p, s = net.place[q]
        lhs = lhs_of(c, q)
        net.arrived(c, q, 2, 3, 4, 5)
        for k in range(4):
            part = product(lhs, w_ref, q, p, k)
            net.r2a[c, q, k, 0] += net.r2b[c, q, k, 0] + part[:, :128]
            net.r2a[c, q, k, 1] += net.r2b[c, q, k, 1] + part[:, 128:]
        net.send(c, q, 6, 7, 8, 9)
        net.sent(c, q, 0, 1)

    def relay_second(c, q):
        p, s = net.place[q]
        net.arrived(c, q, 6)
        net.r3[c, q, 0] += net.r2a[c, q, plus(s, 1), 0]
        net.send(c, q, 10)
        net.arrived(c, q, 7)
        net.r3[c, q, 1] += net.r2a[c, q, plus(s, -1), 1]
        net.send(c, q, 11)

    def own_second(c, q):
        p, s = net.place[q]
        net.sent(c, q, 2, 3, 4, 5)
        net.arrived(c, q, 8, 9, 10, 11)
        for half in range(2):
            total = net.r2a[c, q, s, half] + net.r4[c, q, 0, half] + net.r4[c, q, 1, half]
            finish(c, q, half, total)
        net.send(c, q, 12, 13, 14, 15)

    def forward_first(c, q):
        net.sent(c, q, 6, 7, 8, 9, 10, 11)
        net.arrived(c, q, 12)
        net.send(c, q, 16)
        net.arrived(c, q, 13)
        net.send(c, q, 17)

    def send_second(c, q):
        net.arrived(c, q, 14, 15, 16, 17)
        net.send(c, q, 18, 19, 20, 21)

    def forward_second(c, q):
        net.arrived(c, q, 18)
        net.send(c, q, 22)
        net.arrived(c, q, 19)
        net.send(c, q, 23)

    for body in (relay_first, own_first, relay_second, own_second, forward_first, send_second, forward_second):
        over_chunks(body)


def stage_tail(net, c, q):
    net.arrived(c, q, 20, 21, 22, 23)
    net.sent(c, q, 12, 13, 14, 15, 16, 17, 18, 19, 20, 21, 22, 23)


def normed(net, c, q, gain_ref):
    rows = net.xg.shape[-2]
    tile = 16 if rows % 16 == 0 else 8

    @pl.loop(0, rows // tile)
    def _(i):
        span = pl.ds(pl.multiple_of(i * tile, tile), tile)
        acts = [net.xg[c, q, first, second, half, span].astype(F32) for first in range(4) for second in range(4) for half in range(2)]
        squares = functools.reduce(jnp.add, [v * v for v in acts])
        inv = lax.rsqrt(jnp.sum(squares, axis=-1, keepdims=True) * (1.0 / (128 * len(acts))) + EPS)
        for k, v in enumerate(acts):
            net.xg[c, q, k // 8, (k // 2) % 4, k % 2, span] = (v * inv * gain_ref[q, pl.ds(k, 1)]).astype(BF16)


def rows_of(net, c, q):
    parts = []
    for block in range(16):
        first, second = (block % 4, block // 4) if q == 0 else (block // 4, block % 4)
        parts += [net.xg[c, q, first, second, 0], net.xg[c, q, first, second, 1]]
    return jnp.concatenate(parts, axis=1)


def mega_kernel(chunks, a_ref, res_ref, gain_ref, next_gain_ref, w_out_hbm, w_gate_hbm, w_up_hbm, w_down_hbm,
                h_hbm, new_res_ref,
                w_out, w_gate, w_up, w_down, inner, res2, st2, sb, r1, r2a, r2b, r3, r4, xg,
                w_sem, out_sem, send_sem, recv_sem):
    loads = [pltpu.make_async_copy(src, dst, w_sem.at[i]) for i, (src, dst) in enumerate(
        ((w_out_hbm, w_out), (w_gate_hbm, w_gate), (w_up_hbm, w_up), (w_down_hbm, w_down)))]
    for load in loads:
        load.start()
    net = Torus((st2, sb, r1, r2a, r2b, r3, r4, xg), send_sem, recv_sem)
    net.barrier()
    loads[0].wait()

    @pl.loop(0, chunks)
    def _(c):
        for q in range(2):
            stage_head(net, c, q, a_ref[c, q], w_out)

    def finish_attention(c, q, half, total):
        p, s = net.place[q]
        value = (res_ref[c, q, half].astype(F32) + total).astype(BF16)
        res2[c, q, half] = value
        xg[c, q, p, s, half] = value

    stage_rest(net, chunks, lambda c, q: a_ref[c, q], w_out, finish_attention)
    for load in loads[1:]:
        load.wait()

    @pl.loop(0, chunks)
    def _(c):
        for q in range(2):
            stage_tail(net, c, q)
            normed(net, c, q, gain_ref)
            rows = rows_of(net, c, q)
            gate = lax.dot_general(rows, w_gate[...], (((1,), (1,)), ((), ())), preferred_element_type=F32)
            up = lax.dot_general(rows, w_up[...], (((1,), (1,)), ((), ())), preferred_element_type=F32)
            inner[c, q] = (jax.nn.silu(gate) * up).astype(BF16)
            stage_head(net, c, q, inner[c, q], w_down)

    def finish_mlp(c, q, half, total):
        p, s = net.place[q]
        value = (res2[c, q, half].astype(F32) + total).astype(BF16)
        new_res_ref[c, q, half] = value
        xg[c, q, p, s, half] = value

    stage_rest(net, chunks, lambda c, q: inner[c, q], w_down, finish_mlp)

    def out_copy(c, q):
        return pltpu.make_async_copy(xg.at[c, q], h_hbm.at[c, q], out_sem.at[c, q])

    @pl.loop(0, chunks)
    def _(c):
        for q in range(2):
            stage_tail(net, c, q)
            normed(net, c, q, next_gain_ref)
            out_copy(c, q).start()

    @pl.loop(0, chunks)
    def _(c):
        for q in range(2):
            out_copy(c, q).wait()


def mega(a, res, gain, next_gain, w_out, w_gate_t, w_up_t, w_down, collective_id):
    chunks, _, rows, depth = a.shape
    hidden = w_gate_t.shape[0]
    width = w_out.shape[1]
    per = (chunks, 2)
    vmem = pl.BlockSpec(memory_space=pltpu.VMEM)
    hbm = pl.BlockSpec(memory_space=pl.ANY)

    def by_color(g):
        grid = g.reshape(4, 4, 2, 128)
        return jnp.stack([grid.transpose(1, 0, 2, 3), grid]).reshape(2, 32, 128)

    return pl.pallas_call(
        functools.partial(mega_kernel, chunks),
        out_shape=(jax.ShapeDtypeStruct(per + (4, 4, 2, rows, 128), BF16), jax.ShapeDtypeStruct(per + (2, rows, 128), BF16)),
        in_specs=[vmem] * 4 + [hbm] * 4,
        out_specs=(hbm, vmem),
        scratch_shapes=[
            pltpu.VMEM((depth, width), BF16),
            pltpu.VMEM((hidden, width), BF16),
            pltpu.VMEM((hidden, width), BF16),
            pltpu.VMEM((hidden, width), BF16),
            pltpu.VMEM(per + (rows, hidden), BF16),
            pltpu.VMEM(per + (2, rows, 128), BF16),
            pltpu.VMEM(per + (4, 2, rows, 128), F32),
            pltpu.VMEM(per + (2, 2, 2, rows, 128), F32),
            pltpu.VMEM(per + (2, 2, 2, rows, 128), F32),
            pltpu.VMEM(per + (4, 2, rows, 128), F32),
            pltpu.VMEM(per + (4, 2, rows, 128), F32),
            pltpu.VMEM(per + (2, rows, 128), F32),
            pltpu.VMEM(per + (2, 2, rows, 128), F32),
            pltpu.VMEM(per + (4, 4, 2, rows, 128), BF16),
            pltpu.SemaphoreType.DMA((4,)),
            pltpu.SemaphoreType.DMA(per),
            pltpu.SemaphoreType.DMA(per + (N_KINDS,)),
            pltpu.SemaphoreType.DMA(per + (N_KINDS,)),
        ],
        compiler_params=pltpu.CompilerParams(collective_id=collective_id, has_side_effects=True, vmem_limit_bytes=67_000_000),
        name=f"mega{collective_id}",
    )(a, res, by_color(gain), by_color(next_gain), w_out, w_gate_t, w_up_t, w_down)


from jax.sharding import PartitionSpec as P

ROPE_BASE = 10000.0


def rms_norm(acts_in, gain_vec):
    acts_f = acts_in.astype(F32)
    inv_rms = lax.rsqrt(jnp.mean(acts_f * acts_f, axis=-1, keepdims=True) + EPS)
    return (acts_f * inv_rms * gain_vec).astype(BF16)


def rope_tables(positions, half_dim):
    frequency = ROPE_BASE ** (-jnp.arange(half_dim, dtype=F32) / half_dim)
    angles = positions.astype(F32)[..., None] * frequency
    return jnp.cos(angles)[..., None, :], jnp.sin(angles)[..., None, :]


def rotary(projected, tables):
    cos_part, sin_part = tables
    half_dim = projected.shape[-1] // 2
    lower_half = projected[..., :half_dim]
    upper_half = projected[..., half_dim:]
    return jnp.concatenate([lower_half * cos_part - upper_half * sin_part, upper_half * cos_part + lower_half * sin_part], axis=-1)


def attend(queries, keys, values, query_pos, key_pos):
    head_dim = queries.shape[-1]
    scores = jnp.einsum('the,she->hts', queries, keys, preferred_element_type=F32) * (head_dim ** -0.5)
    visible = (key_pos[None, :] <= query_pos[:, None])[None]
    scores = jnp.where(visible, scores, -jnp.inf)
    row_max = jnp.max(scores, axis=-1, keepdims=True)
    exp_scores = jnp.exp(scores - row_max)
    row_sum = jnp.moveaxis(jnp.sum(exp_scores, axis=-1), -1, 0)
    mixed = jnp.einsum('hts,she->the', exp_scores.astype(BF16), values, preferred_element_type=F32)
    return (mixed / row_sum[..., None]).astype(BF16)


def solution(mesh):
    groups = mesh.shape['resp']
    row_axes = ('prompts', 'resp')
    head_spec = P(None, None, 'model', None)
    in_specs = (P(row_axes, None), P(row_axes, None, None), P(row_axes, None), P(row_axes), P(None, None), head_spec, head_spec, head_spec, P(None, 'model', None, None), P(None, None), P(None, None, 'model'), P(None, None, 'model'), P(None, 'model', None), P(None), P(None, 'model'))
    chunks = 4

    def device_step(x_prompt, x_resp, targets, resp_lens, attn_gain, w_query, w_key, w_value, w_out, mlp_gain, w_gate, w_up, w_down, final_gain, w_vocab):
        prompt_rows = x_prompt.shape[0]
        resp_len, width = x_resp.shape[1:]
        prompt_len = prompt_rows * groups
        num_layers, _, heads, head_dim = w_query.shape
        me = lax.axis_index('model')
        resp_pos = prompt_len + jnp.arange(resp_len)
        tok_pos = jnp.concatenate([lax.axis_index('resp') * prompt_rows + jnp.arange(prompt_rows), resp_pos])
        key_pos = jnp.concatenate([jnp.arange(prompt_len), resp_pos])
        rows = jnp.concatenate([x_prompt, x_resp[0]], axis=0)
        residual = lax.dynamic_slice_in_dim(rows, me * 256, 256, 1)
        hidden = rms_norm(rows, attn_gain[0])
        gate_t, up_t = jnp.swapaxes(w_gate, 1, 2), jnp.swapaxes(w_up, 1, 2)

        for layer_idx in range(num_layers):
            tables = rope_tables(tok_pos, head_dim // 2)
            keys = rotary(jnp.einsum('td,dhe->the', hidden, w_key[layer_idx], preferred_element_type=F32), tables).astype(BF16)
            values = jnp.einsum('td,dhe->the', hidden, w_value[layer_idx], preferred_element_type=F32).astype(BF16)
            both = lax.all_gather(jnp.concatenate([keys[:prompt_rows], values[:prompt_rows]], axis=1), 'resp', axis=0, tiled=True)
            all_keys = jnp.concatenate([both[:, :heads], keys[prompt_rows:]], axis=0)
            all_values = jnp.concatenate([both[:, heads:], values[prompt_rows:]], axis=0)
            query_pos = tok_pos
            last = layer_idx == num_layers - 1
            if last:
                residual = residual[prompt_rows:]
                hidden = hidden[prompt_rows:]
                query_pos = resp_pos
                tables = rope_tables(query_pos, head_dim // 2)
            queries = rotary(jnp.einsum('td,dhe->the', hidden, w_query[layer_idx], preferred_element_type=F32), tables).astype(BF16)
            mixed = attend(queries, all_keys, all_values, query_pos, key_pos)
            count = residual.shape[0]
            part = count // (2 * chunks)
            gathered, new_res = mega(
                mixed.reshape(chunks, 2, part, heads * head_dim),
                residual.reshape(chunks, 2, part, 2, 128).transpose(0, 1, 3, 2, 4),
                mlp_gain[layer_idx], final_gain if last else attn_gain[layer_idx + 1],
                w_out[layer_idx].reshape(heads * head_dim, width), gate_t[layer_idx], up_t[layer_idx], w_down[layer_idx], layer_idx)
            residual = new_res.transpose(0, 1, 3, 2, 4).reshape(count, 256)
            first = gathered[:, 0].transpose(0, 4, 2, 1, 3, 5).reshape(chunks, part, width)
            second = gathered[:, 1].transpose(0, 4, 1, 2, 3, 5).reshape(chunks, part, width)
            hidden = jnp.stack([first, second], axis=1).reshape(count, width)
        logits = jnp.dot(hidden, w_vocab, preferred_element_type=F32)
        vocab_local = logits.shape[-1]
        vocab_ids = me * vocab_local + jnp.arange(vocab_local)
        row_max = jnp.max(logits, axis=-1)
        exp_total = jnp.sum(jnp.exp(logits - row_max[:, None]), axis=-1)
        picked = jnp.sum(jnp.where(vocab_ids[None, :] == targets[0][:, None], logits, 0.0), axis=-1)
        stats = lax.all_gather(jnp.stack([row_max, exp_total, picked]), 'model', axis=0)
        top = jnp.max(stats[:, 0], axis=0)
        total = jnp.sum(stats[:, 1] * jnp.exp(stats[:, 0] - top), axis=0)
        log_probs = jnp.sum(stats[:, 2], axis=0) - top - jnp.log(total)
        log_probs = jnp.where(jnp.arange(resp_len) < resp_lens[0], log_probs, 0.0)
        return log_probs[None, :]

    return jax.shard_map(device_step, mesh=mesh, in_specs=in_specs, out_specs=P(row_axes, None), check_vma=False)
```

time: 1100 us -> 964 us (0.88)
  waiting for transfers between devices: 769 us -> 13.8 us
  Pallas kernels: 0 us -> 570 us
  local copies, waits for them, and re-layouts: 63.4 us -> 174 us
  matrix products: 167 us -> 94.3 us
    pallas_call x0 -> x2, Pallas kernels: none -> 570 us  [mega(): pl.pallas_call(functools.partial(mega_kernel, chunks), out_shape=(jax.Sha...]
    all_gather x6 -> x2, waiting for transfers between devices: 309 us -> 13.7 us  [device_step(): lax.all_gather(jnp.concatenate([keys[:prompt_rows], values[:prompt_rows]]...]
    unnamed x12 -> x2, waiting for transfers between devices: 240 us -> 0.03 us
    reduce_scatter x2 -> x0, waiting for transfers between devices: 220 us -> none  [reduce_rows(): return lax.psum_scatter(part, 'model', scatter_dimension=0, tiled=True)]
    dot_general x13 -> x5, matrix products: 128 us -> 59.1 us  [the longest x2 25.6 us: attend(): jnp.einsum('hts,she->the', exp_scores.astype(BF16), values, preferred_ele...]
    transpose x0 -> x8, local copies, waits for them, and re-layouts: none -> 48.5 us  [the longest x4 31.6 us: device_step(): gathered[:, 0].transpose(0, 4, 2, 1, 3, 5).reshape(chunks, part, width)]
    another operation x0 -> x7, local copies, waits for them, and re-layouts: none -> 38.9 us  [the longest x4 38.2 us: device_step(): hidden = jnp.stack([first, second], axis=1).reshape(count, width)]
    squeeze x0 -> x2, local copies, waits for them, and re-layouts: none -> 27.3 us  [the longest x1 17.1 us: device_step(): up_t[layer_idx]]
  transfers between devices with their start and end apart: 10 -> 2, of which waited for: 9 -> 1; matrix products, arithmetic and copies ran while one was open for 4% -> 7% of each run, Pallas kernels for 0% -> 0%
where the time goes in v2:
time: 964 us; the launch traced here: 946 us
  Pallas kernels  570 us (59%)
  local copies, waits for them, and re-layouts  174 us (18%)
  matrix products  94.3 us (10%)
  other arithmetic  60.8 us (6%)
  blocking collectives  18.1 us (2%)
  between operations  15 us (2%)
  waiting for transfers between devices  13.8 us (1%)
    pallas_call x2, Pallas kernels, mega(): pl.pallas_call(functools.partial(mega_kernel, chunks), out_shape=(jax.Sha...  570 us
    another operation x4, local copies, waits for them, and re-layouts, device_step(): hidden = jnp.stack([first, second], axis=1).reshape(count, width)  38.2 us
    transpose x4, local copies, waits for them, and re-layouts, device_step(): gathered[:, 0].transpose(0, 4, 2, 1, 3, 5).reshape(chunks, part, width)  31.6 us
    dot_general x2, matrix products, attend(): jnp.einsum('hts,she->the', exp_scores.astype(BF16), values, preferred_ele...  25.6 us
    unnamed x59, local copies, waits for them, and re-layouts  25.6 us
    dot_general x1, matrix products, device_step(): logits = jnp.dot(hidden, w_vocab, preferred_element_type=F32)  23.3 us
    unnamed x4, matrix products  21.6 us
  transfers between devices with their start and end apart: 2, of which 1 were waited for; matrix products, arithmetic and copies ran while one was open for 7% of the time, Pallas kernels for 0%

profile of v2, /device:TPU:1, one launch (start us, length us, event | category | flops | bytes accessed | tf_op | source)
XLA Modules:
  0.0 945.8 jit_solution(644705921674117066)
XLA Ops:
  16.1 6.2 copy.127
  22.3 6.1 fusion.95
  28.4 6.2 copy.125
  34.6 10.9 %fusion.2 = bf16[1152,4096]{1,0:T(8,128)(2,1)} fusion(f32[4096]{0:T(1024)S(1)} %bitcast.176, f32[1152]{0:T(1024)S(1)} %add_rsqrt_fusion, bf16[1024,4096]{1,0:T(8,128)(2,1)} %bitcast.145, bf16[128,4096]{1,0:T(8,128)(2,1)S(1)} %copy-done.3), kind=kLoop, calls=%fused_computation.4 | loop fusion | flops 33030144 | bytes 18895360 | tf_op jit(solution)/shard_map/convert_element_type | solution.py:346
  45.4 8.4 fusion.102
  57.8 5.9 fusion.94
  63.7 6.8 fusion.22
  81.2 10.2 %slice_bitcast_fusion.4 = (bf16[688,4096]{1,0:T(8,128)(2,1)}, bf16[688,4096]{1,0:T(8,128)(2,1)}) fusion(bf16[2,688,4096]{2,1,0:T(8,128)(2,1)} %param.27), kind=kLoop, calls=%fused_computation.34 | loop fusion | bytes 22544384 | tf_op jit(solution)/shard_map/squeeze | solution.py:418
  100.0 6.2 copy.128
  110.9 17.1 %slice_bitcast_fusion = (bf16[688,4096]{1,0:T(8,128)(2,1)}, bf16[688,4096]{1,0:T(8,128)(2,1)}, bf16[688,4096]{1,0:T(8,128)(2,1)}, bf16[688,4096]{1,0:T(8,128)(2,1)}) fusion(bf16[2,688,4096]{2,1,0:T(8,128)(2,1)} %bitcast.149, bf16[2,688,4096]{2,1,0:T(8,128)(2,1)} %bitcast.150), kind=kLoop, calls=%fused_computation.30 | loop fusion | bytes 45088768 | tf_op jit(solution)/shard_map/squeeze | solution.py:418
  135.4 5.8 fusion.5
  141.8 18.6 %fusion.28 = bf16[1152,2,128]{0,2,1:T(8,128)(2,1)S(1)} fusion(f32[2,1152,2048]{2,1,0:T(8,128)} %copy-done, f32[2,1152]{1,0:T(2,128)S(1)} %get-tuple-element.59, pred[1152,2048]{1,0:T(8,128)(4,1)S(1)} %broadcast_compare_fusion, bf16[1024,2,128]{0,2,1:T(8,128)(2,1)S(1)} %slice-done, bf16[1024,2,128]{0,2,1:T(8,128)(2,1)} %get-tuple-element.43, ...), kind=kOutput, calls=%fused_computation.46 | convolution fusion | flops 1229520896 | bytes 22890496 | tf_op jit(solution)/shard_map/hts,she->the/dot_general | solution.py:371
  162.2 300.9 %mega0.1 = (bf16[4,2,4,4,2,144,128]{6,5,4,3,2,1,0:T(8,128)(2,1)}, bf16[4,2,2,144,128]{4,3,2,1,0:T(8,128)(2,1)}) custom-call(bf16[4,2,144,256]{3,2,1,0:T(8,128)(2,1)} %reshape.270.a_ref, bf16[4,2,2,144,128]{4,3,2,1,0:T(8,128)(2,1)} %bitcast.157, f32[2,32,128]{2,1,0:T(8,128)} %get-tuple-element.67.gain_ref, f32[2,32,128]{2,1,0:T(8,128)} %get-tuple-element.68.next_gain_ref, ...), custom_call_target="tpu_custom_call" | custom-call | tf_op jit(solution)/shard_map/mega0/pallas_call | solution.py:308
  463.1 10.0 %slice_bitcast_fusion.7 = (bf16[4,144,4,4,2,128]{5,1,4,2,3,0:T(8,128)(2,1)}, bf16[4,144,4,4,2,128]{5,1,4,3,2,0:T(8,128)(2,1)}) fusion(bf16[4,2,4,4,2,144,128]{6,5,4,3,2,1,0:T(8,128)(2,1)} %get-tuple-element.8), kind=kLoop, calls=%fused_computation.37 | loop fusion | bytes 18874368 | tf_op jit(solution)/shard_map/transpose | solution.py:420
  473.1 8.2 copy.99
  481.3 8.8 stack_reshape.13
  490.1 8.1 copy.100
  498.3 9.2 stack_reshape.14
  507.5 8.3 pad_maximum_fusion.1
  515.7 8.9 copy.101
  524.6 6.7 convolution_convert_fusion
  542.3 6.4 fusion.14
  549.7 13.7 %all-gather.7.cloned.1.call-done = bf16[1024,4,128]{0,2,1:T(8,128)(2,1)} async-done(((bf16[128,4,128]{0,2,1:T(8,128)(2,1)}), bf16[1024,4,128]{0,2,1:T(8,128)(2,1)}) %all-gather.7.cloned.1.call-update) | async-done | bytes 1048592 | tf_op jit(solution)/shard_map/all_gather | solution.py:400
  575.7 7.1 divide_convert_fusion
  585.5 268.6 %mega1.1 = (bf16[4,2,4,4,2,128,128]{6,5,4,3,2,1,0:T(8,128)(2,1)}, bf16[4,2,2,128,128]{4,3,2,1,0:T(8,128)(2,1)}) custom-call(bf16[4,2,128,256]{3,2,1,0:T(8,128)(2,1)} %copy.123.a_ref, bf16[4,2,2,128,128]{4,3,2,1,0:T(8,128)(2,1)} %bitcast.160, f32[2,32,128]{2,1,0:T(8,128)} %get-tuple-element.69.gain_ref, f32[2,32,128]{2,1,0:T(8,128)} %get-tuple-element.70.next_gain_ref, ...), custom_call_target="tpu_custom_call" | custom-call | tf_op jit(solution)/shard_map/mega1/pallas_call | solution.py:308
  854.1 6.1 slice_bitcast_fusion.9
  860.1 7.3 copy.113
  867.4 7.3 copy.114
  874.7 7.5 pad_maximum_fusion.2
  882.2 11.4 %copy.115 = bf16[4,2,128,4096]{3,2,1,0:T(8,128)(2,1)} copy(bf16[4,2,128,4096]{2,3,0,1:T(8,128)(2,1)} %pad_maximum_fusion.2) | data formatting | bytes 16777216 | tf_op jit(solution)/shard_map/stack | solution.py:422
  893.6 23.3 %fusion.100 = (f32[1024]{0:T(1024)S(1)}, f32[1024,2048]{1,0:T(8,128)S(1)}) fusion(bf16[1024,4096]{1,0:T(8,128)(2,1)} %bitcast.154, bf16[4096,2048]{1,0:T(8,128)(2,1)} %param.29), kind=kOutput, calls=%fused_computation.145 | convolution fusion | flops 17181966336 | bytes 33558528 | tf_op jit(solution)/shard_map/dot_general | solution.py:423
  919.5 18.1 %all-gather.1 = f32[16,3,1024]{2,1,0:T(4,128)S(1)} all-gather(f32[1,3,1024]{2,1,0:T(4,128)S(1)} %maximum_bitcast_fusion), channel_id=2, replica_groups=mesh['prompts'=1,'model'=16,'resp'=8] {'model'}, dimensions={0}, use_global_device_ids=true | all-gather | bytes 208896 | tf_op jit(solution)/shard_map/all_gather | solution.py:429
  (120 shorter events, 76.6 us)
Async XLA Ops:
  6.5 5.7 copy-start.25
  6.5 121.5 %all-gather.5.cloned.1.call-start = ((), (), s32[]{:S(2)}) async-start(), calls=%async_computation | async-start | bytes 1179648 | tf_op jit(solution)/shard_map/all_gather | solution.py:400
  6.5 5.7 copy-start.4
  22.3 12.3 %copy-start.3 = (bf16[128,4096]{1,0:T(8,128)(2,1)S(1)}, bf16[128,4096]{1,0:T(8,128)(2,1)}, u32[]{:S(2)}) copy-start(bf16[128,4096]{1,0:T(8,128)(2,1)} %param.15) | copy-start | bytes 3145732
  45.4 8.4 copy-start.1
  45.4 8.4 copy-start.10
  63.7 8.7 copy-start.17
  63.7 8.7 copy-start.18
  70.6 3.1 copy-start.20
  71.7 0.7 copy-start.5
  71.7 1.9 copy-start.7
  73.6 0.7 copy-start.12
  75.0 488.4 %all-gather.7.cloned.1.call-start = ((), (), s32[]{:S(2)}) async-start(), calls=%async_computation.1 | async-start | bytes 1179648 | tf_op jit(solution)/shard_map/all_gather | solution.py:400
  96.2 10.1 %copy-start.23 = (f32[4096]{0:T(1024)S(1)}, f32[4096]{0:T(1024)}, u32[]{:S(2)}) copy-start(f32[4096]{0:T(1024)} %param.28) | copy-start | bytes 49156
  110.9 19.2 %copy-start.13 = (bf16[1152,2,64]{0,2,1:T(8,128)(2,1)S(1)}, bf16[1152,2,64]{0,2,1:T(8,128)(2,1)}, u32[]{:S(2)}) copy-start(bf16[1152,2,64]{0,2,1:T(8,128)(2,1)} %copy-done.12) | copy-start | bytes 884740
  110.9 19.2 %copy-start.22 = (bf16[1152,2,64]{0,2,1:T(8,128)(2,1)S(1)}, bf16[1152,2,64]{0,2,1:T(8,128)(2,1)}, u32[]{:S(2)}) copy-start(bf16[1152,2,64]{0,2,1:T(8,128)(2,1)} %get-tuple-element.35) | copy-start | bytes 884740
  135.3 6.4 copy-start
  135.4 6.4 slice-start
  515.7 8.9 copy-start.11
  524.6 6.8 copy-start.2
  524.6 7.0 copy-start.9
  531.3 3.1 copy-start.21
  531.6 2.9 copy-start.6
  531.6 2.9 copy-start.8
  534.7 0.7 copy-start.14
  534.7 0.8 copy-start.16
  542.3 6.4 copy-start.19
  542.3 23.2 %copy-start.15 = (bf16[1152,2,64]{0,2,1:T(8,128)(2,1)S(1)}, bf16[1152,2,64]{0,2,1:T(8,128)(2,1)}, u32[]{:S(2)}) copy-start(bf16[1152,2,64]{0,2,1:T(8,128)(2,1)} %copy-done.14) | copy-start | bytes 884740
  570.5 5.2 slice-start.1
  893.6 23.3 %copy-start.24 = (s32[2048]{0:T(1024)S(1)}, s32[2048]{0:T(1024)}, u32[]{:S(2)}) copy-start(s32[2048]{0:T(1024)} %iota_add_fusion) | copy-start | bytes 24580
  893.6 23.3 %copy-start.26 = (s32[1,1024]{1,0:T(1,128)S(1)}, s32[1,1024]{1,0:T(1,128)}, u32[]{:S(2)}) copy-start(s32[1,1024]{1,0:T(1,128)} %param.17) | copy-start | bytes 12292
Sparse Core Ops, SparseCore 0:
  75.2 26.6 all-gather.4
  536.3 27.0 all-gather.6
